TPU v7x, 32 devices: a whole 2x2x4 slice. The times are simulated.
32 devices in a mesh: row: 4 (over x, core), col: 8 (over z, y).
Axes of the slice: x: 2, y: 2, z: 4, core: 2. Of those that a mesh axis runs over, the one named last changes fastest.
Arguments:
- weight: bfloat16 [16384, 16384], P('row', 'col'), may hold values from -0.046875 to 0.046875
- momentum: float32 [16384, 16384], P('row', 'col'), may hold values from -36 to 36
- right_factor: float32 [16384, 512], P(('col', 'row')), may hold values from -0.046875 to 0.046875
- output_grads: bfloat16 [1024, 16384], P('col', 'row'), may hold values from -0.1875 to 0.1875
- activations: bfloat16 [1024, 16384], P('row', 'col'), may hold values from -6 to 6
Outputs:
- new_weight: bfloat16 [16384, 16384], P('row', 'col')
- new_momentum: float32 [16384, 16384], P('row', 'col')
- new_factor: float32 [16384, 512], P(('col', 'row'))
All inputs are finite; a program needn't handle non-finite values.
Results may differ from a plain program's by a relative error of at most 0.0004.
Values may be sent and summed in bfloat16 or wider, within the bound.
No kernel may reach another device: no remote copies, remote signals or barrier semaphores. Data moves between devices by JAX's collectives and lax.ppermute only.
A program may use at most 192 MiB of HBM per device.

v0:
```python
import math
import jax
import jax.numpy as jnp
from jax import lax
from jax.sharding import PartitionSpec as P

D_OUT = 16384
D_IN = 16384
FULL_PRECISION = lax.Precision.HIGHEST
MOMENTUM_DECAY = 0.95
LEARN_RATE = 0.002
NORM_EPS = 1e-06


def contract_rows(first, second):
    return lax.dot_general(
        first,
        second,
        (((0,), (0,)), ((), ())),
        precision=FULL_PRECISION,
        preferred_element_type=jnp.float32,
    )


def outer_rows(first, second):
    return lax.dot_general(
        first,
        second,
        (((1,), (1,)), ((), ())),
        precision=FULL_PRECISION,
        preferred_element_type=jnp.float32,
    )


def orthogonalize(left_factor, gram_matrix):
    lower_factor = jnp.linalg.cholesky(gram_matrix)
    identity = jnp.eye(gram_matrix.shape[0], dtype=gram_matrix.dtype)
    inverse = jax.scipy.linalg.solve_triangular(lower_factor, identity, lower=True)
    return outer_rows(left_factor, inverse)


def body(weight, momentum, right_factor, output_grads, activations):
    grads_whole = lax.all_gather(output_grads, "col", axis=0, tiled=True)
    grad_tile = lax.dot_general(
        grads_whole,
        lax.all_gather(activations, "row", axis=0, tiled=True),
        (((0,), (0,)), ((), ())),
        preferred_element_type=jnp.float32,
    )
    buffer = momentum + grad_tile
    factor_block = lax.all_gather(right_factor, "row", axis=0, tiled=True)
    left_partial = jnp.dot(
        buffer, factor_block, precision=FULL_PRECISION, preferred_element_type=jnp.float32
    )
    left_factor = lax.psum(left_partial, "col")
    gram_matrix = lax.psum(contract_rows(left_factor, left_factor), "row")
    ortho_left = orthogonalize(left_factor, gram_matrix)
    right_piece = lax.psum_scatter(
        contract_rows(buffer, ortho_left), "row", scatter_dimension=0, tiled=True
    )
    column_squares = lax.psum(jnp.sum(right_piece * right_piece, axis=0), ("row", "col"))
    column_norm = jnp.sqrt(column_squares + NORM_EPS)
    new_factor = right_piece / column_norm
    projected = lax.all_gather(right_piece, "row", axis=0, tiled=True)
    new_momentum = buffer - (1.0 - MOMENTUM_DECAY) * outer_rows(ortho_left, projected)
    factor_cols = projected / column_norm
    step_scale = LEARN_RATE * math.sqrt(max(D_OUT, D_IN))
    new_weight = (
        weight.astype(jnp.float32) - step_scale * outer_rows(ortho_left, factor_cols)
    ).astype(jnp.bfloat16)
    return (new_weight, new_momentum, new_factor)


def solution(mesh):
    in_specs = (
        P("row", "col"),
        P("row", "col"),
        P(("col", "row"), None),
        P("col", "row"),
        P("row", "col"),
    )
    out_specs = (P("row", "col"), P("row", "col"), P(("col", "row"), None))
    return jax.shard_map(body, mesh=mesh, in_specs=in_specs, out_specs=out_specs, check_vma=False)
```

profile of v0, /device:TPU:0, one launch (start us, length us, event | category | flops | bytes accessed | tf_op | source)
XLA Modules:
  0.0 1043.1 jit_solution(17681060143477142184)
XLA Ops:
  9.4 37.3 %all-gather.7.cloned.1.call-done = bf16[1024,2048]{1,0:T(8,128)(2,1)} async-done(((bf16[256,2048]{1,0:T(8,128)(2,1)}), bf16[1024,2048]{1,0:T(8,128)(2,1)}) %all-gather.7.cloned.1.call-update) | async-done | bytes 4194320 | tf_op jit(solution)/shard_map/all_gather | solution.py:46
  46.7 126.6 %all-gather.5.cloned.1.call-done = bf16[1024,4096]{1,0:T(8,128)(2,1)} async-done(((bf16[128,4096]{1,0:T(8,128)(2,1)}), bf16[1024,4096]{1,0:T(8,128)(2,1)}) %all-gather.5.cloned.1.call-update) | async-done | bytes 8388624 | tf_op jit(solution)/shard_map/all_gather | solution.py:43
  173.4 36.2 %convolution_add_fusion = f32[4096,2048]{1,0:T(8,128)} fusion(f32[4096,2048]{1,0:T(8,128)} %param.6, bf16[1024,4096]{1,0:T(8,128)(2,1)} %all-gather.5.cloned.1.call-done, bf16[1024,2048]{1,0:T(8,128)(2,1)} %all-gather.7.cloned.1.call-done), kind=kOutput, calls=%fused_computation.4 | convolution fusion | flops 17188257792 | bytes 79691776 | tf_op jit(solution)/shard_map/dot_general | solution.py:44
  209.6 65.1 %fusion.43 = f32[4096,512]{1,0:T(8,128)} fusion(f32[4096,2048]{1,0:T(8,128)} %convolution_add_fusion, f32[2048,512]{1,0:T(8,128)} %all-gather.9.cloned.1.call-done), kind=kOutput, calls=%fused_computation.85 | convolution fusion | flops 51539607552 | bytes 46137344 | tf_op jit(solution)/shard_map/dot_general | solution.py:52
  275.0 267.8 %all-reduce.4.cloned.1.call-done = f32[4096,512]{1,0:T(8,128)} async-done(((f32[4096,512]{1,0:T(8,128)}), f32[4096,512]{1,0:T(8,128)}) %all-reduce.4.cloned.1.call-update) | async-done | bytes 8388624 | tf_op jit(solution)/shard_map/psum | solution.py:55
  542.8 18.5 %fusion.44 = f32[512,512]{0,1:T(8,128)} fusion(f32[4096,512]{1,0:T(8,128)} %all-reduce.4.cloned.1.call-done), kind=kOutput, calls=%fused_computation.86 | convolution fusion | flops 12884901888 | bytes 9437184 | tf_op jit(solution)/shard_map/dot_general | solution.py:16
  562.3 34.6 %all-reduce.6.cloned.1.call-done = f32[512,512]{0,1:T(8,128)} async-done(((f32[512,512]{0,1:T(8,128)}), f32[512,512]{0,1:T(8,128)}) %all-reduce.6.cloned.1.call-update) | async-done | bytes 1048592 | tf_op jit(solution)/shard_map/psum | solution.py:56
  599.9 11.7 %cholesky.104 = f32[128,128]{1,0:T(8,128)S(1)} custom-call(f32[128,128]{1,0:T(8,128)S(1)} %cholesky.266), custom_call_target="Cholesky" | custom-call | tf_op jit(solution)/shard_map/jit(cholesky)/cholesky | solution.py:36
  611.7 9.8 custom-call.31
  622.3 11.7 %cholesky.217 = f32[128,128]{1,0:T(8,128)S(1)} custom-call(f32[128,128]{1,0:T(8,128)S(1)} %cholesky.270), custom_call_target="Cholesky" | custom-call | tf_op jit(solution)/shard_map/jit(cholesky)/cholesky | solution.py:36
  634.0 18.5 %custom-call.32 = f32[1,128,128]{1,2,0:T(8,128)S(1)} custom-call(f32[1,128,128]{2,1,0:T(8,128)S(1)} %get-tuple-element.27), custom_call_target="InvertDiagBlocksLowerTriangular" | custom-call | tf_op jit(solution)/shard_map/jit(cholesky)/cholesky | solution.py:36
  653.2 11.7 %cholesky.238 = f32[128,128]{1,0:T(8,128)S(1)} custom-call(f32[128,128]{1,0:T(8,128)S(1)} %cholesky.275), custom_call_target="Cholesky" | custom-call | tf_op jit(solution)/shard_map/jit(cholesky)/cholesky | solution.py:36
  665.6 9.8 custom-call.33
  676.0 11.7 %cholesky.255 = f32[128,128]{1,0:T(8,128)S(1)} custom-call(f32[128,128]{1,0:T(8,128)S(1)} %convolution_subtract_fusion.5), custom_call_target="Cholesky" | custom-call | tf_op jit(solution)/shard_map/jit(cholesky)/cholesky | solution.py:36
  692.0 10.1 while.1
  702.1 40.1 %custom-call.34 = f32[4,128,128]{1,2,0:T(8,128)S(1)} custom-call(f32[4,128,128]{2,1,0:T(8,128)} %get-tuple-element.10), custom_call_target="InvertDiagBlocksLowerTriangular" | custom-call | tf_op jit(solution)/shard_map/jit(_solve_triangular)/triangular_solve | solution.py:38
  746.0 17.1 %fusion.2 = f32[4096,512]{1,0:T(8,128)S(1)} fusion(f32[4096,512]{1,0:T(8,128)} %all-reduce.4.cloned.1.call-done, f32[128,512]{1,0:T(8,128)S(1)} %fusion.30, f32[128,512]{1,0:T(8,128)S(1)} %fusion.31, f32[128,512]{1,0:T(8,128)S(1)} %fusion.33, f32[128,512]{1,0:T(8,128)S(1)} %fusion.21), kind=kOutput, calls=%fused_computation.16 | convolution fusion | flops 12885688320 | bytes 17825792 | tf_op jit(solution)/shard_map/dot_general | solution.py:26
  763.2 3.2 copy-done
  766.4 58.7 %fusion.45 = f32[2048,512]{1,0:T(8,128)} fusion(f32[4096,2048]{1,0:T(8,128)} %convolution_add_fusion, f32[4096,512]{1,0:T(8,128)S(1)} %fusion.2), kind=kOutput, calls=%fused_computation.87 | convolution fusion | flops 51539607552 | bytes 46137344 | tf_op jit(solution)/shard_map/dot_general | solution.py:16
  825.2 45.2 %reduce-scatter.2.cloned.1.call-done = f32[512,512]{1,0:T(8,128)} async-done(((f32[2048,512]{1,0:T(8,128)}), f32[512,512]{1,0:T(8,128)}) %reduce-scatter.2.cloned.1.call-update) | async-done | bytes 1048592 | tf_op jit(solution)/shard_map/reduce_scatter | solution.py:58
  871.7 39.7 %psum.23 = f32[512]{0:T(512)S(1)} all-reduce(f32[512]{0:T(512)S(1)} %multiply_reduce_fusion), channel_id=1, replica_groups=mesh['row'=4,'col'=8] {'row','col'}, use_global_device_ids=true, to_apply=%region_12.13 | all-reduce | flops 512 | bytes 4096 | tf_op jit(solution)/shard_map/psum | solution.py:61
  911.4 2.3 broadcast_divide_fusion
  913.8 62.5 %multiply_subtract_fusion = f32[4096,2048]{1,0:T(8,128)} fusion(f32[4096,2048]{1,0:T(8,128)} %convolution_add_fusion, f32[4096,512]{1,0:T(8,128)} %copy-done, f32[2048,512]{1,0:T(8,128)} %all-gather.11.cloned.1.call-done), kind=kOutput, calls=%fused_computation.2 | convolution fusion | flops 51556384768 | bytes 79691776 | tf_op jit(solution)/shard_map/dot_general | solution.py:26
  976.3 59.6 %subtract_convert_fusion = bf16[4096,2048]{1,0:T(8,128)(2,1)} fusion(bf16[4096,2048]{1,0:T(8,128)(2,1)} %param.5, f32[4096,512]{1,0:T(8,128)} %copy-done, f32[2048,512]{1,0:T(8,128)S(1)} %copy-done.1, f32[512]{0:T(512)S(1)} %add_sqrt_fusion), kind=kOutput, calls=%fused_computation.3 | convolution fusion | flops 51574210560 | bytes 46139392 | tf_op jit(solution)/shard_map/dot_general | solution.py:26
  (65 shorter events, 26.3 us)
Async XLA Ops:
  7.2 39.6 %all-gather.7.cloned.1.call-start = ((), (), s32[]{:S(2)}) async-start(), calls=%async_computation.2 | async-start | bytes 5242880 | tf_op jit(solution)/shard_map/all_gather | solution.py:46
  7.9 165.5 %all-gather.5.cloned.1.call-start = ((), (), s32[]{:S(2)}) async-start(), calls=%async_computation.1 | async-start | bytes 9437184 | tf_op jit(solution)/shard_map/all_gather | solution.py:43
  8.6 201.0 %all-gather.9.cloned.1.call-start = ((), (), s32[]{:S(2)}) async-start(), calls=%async_computation.3 | async-start | bytes 5242880 | tf_op jit(solution)/shard_map/all_gather | solution.py:51
  9.4 533.4 %all-reduce.4.cloned.1.call-start = ((), (), s32[]{:S(2)}) async-start(), calls=%async_computation.4 | async-start | bytes 16777216 | tf_op jit(solution)/shard_map/psum | solution.py:55
  274.7 322.2 %all-reduce.6.cloned.1.call-start = ((), (), s32[]{:S(2)}) async-start(), calls=%async_computation.5 | async-start | bytes 2097152 | tf_op jit(solution)/shard_map/psum | solution.py:56
  561.3 309.0 %reduce-scatter.2.cloned.1.call-start = ((), (), s32[]{:S(2)}) async-start(), calls=%async_computation.6 | async-start | bytes 5242880 | tf_op jit(solution)/shard_map/reduce_scatter | solution.py:58
  763.2 3.2 copy-start
  825.1 88.6 %all-gather.11.cloned.1.call-start = ((), (), s32[]{:S(2)}) async-start(), calls=%async_computation.7 | async-start | bytes 5242880 | tf_op jit(solution)/shard_map/all_gather | solution.py:64
  913.8 62.5 %copy-start.1 = (f32[2048,512]{1,0:T(8,128)S(1)}, f32[2048,512]{1,0:T(8,128)}, u32[]{:S(2)}) copy-start(f32[2048,512]{1,0:T(8,128)} %all-gather.11.cloned.1.call-done) | copy-start | bytes 12582916
Sparse Core Ops, SparseCore 0:
  9.5 37.1 all-gather.6
  48.9 124.4 all-gather.4
  174.9 32.6 all-gather.8
  274.8 267.9 all-reduce.3
  561.5 35.3 all-reduce.5
  825.3 45.0 reduce-scatter.1
  871.9 34.7 all-gather.10
where the time goes:
time: 1050 us; the launch traced here: 1040 us
  waiting for transfers between devices  514 us (49%)
  matrix products  323 us (31%)
  other arithmetic  134 us (13%)
  blocking collectives  39.7 us (4%)
  between operations  17.2 us (2%)
  local copies, waits for them, and re-layouts  15 us (1%)
    psum x1, waiting for transfers between devices, body(): left_factor = lax.psum(left_partial, 'col')  268 us
    dot_general x3, matrix products, outer_rows(): lax.dot_general(first, second, (((1,), (1,)), ((), ())), precision=FULL_P...  139 us
    all_gather x1, waiting for transfers between devices, body(): grads_whole = lax.all_gather(output_grads, 'col', axis=0, tiled=True)  127 us
    another operation x14, other arithmetic, orthogonalize(): lower_factor = jnp.linalg.cholesky(gram_matrix)  87.4 us
    dot_general x2, matrix products, contract_rows(): lax.dot_general(first, second, (((0,), (0,)), ((), ())), precision=FULL_P...  77.2 us
    dot_general x1, matrix products, body(): jnp.dot(buffer, factor_block, precision=FULL_PRECISION, preferred_element...  65.1 us
    reduce_scatter x1, waiting for transfers between devices, body(): lax.psum_scatter(contract_rows(buffer, ortho_left), 'row', scatter_dimens...  45.2 us
    another operation x3, other arithmetic, orthogonalize(): jax.scipy.linalg.solve_triangular(lower_factor, identity, lower=True)  40.3 us
  transfers between devices with their start and end apart: 7, of which 5 were waited for; matrix products, arithmetic and copies ran while one was open for 4% of the time, Pallas kernels for 0%

commit v1 on v0

--- a/solution.py
+++ b/solution.py
@@ -40,7 +40,12 @@
 
 
 def body(weight, momentum, right_factor, output_grads, activations):
-    grads_whole = lax.all_gather(output_grads, "col", axis=0, tiled=True)
+    ring = [output_grads]
+    for hop in range(7):
+        ring.append(lax.ppermute(ring[-1], "col", [(dev, (dev + 1) % 8) for dev in range(8)]))
+    grads_whole = jnp.roll(
+        jnp.concatenate(ring[::-1], axis=0), (lax.axis_index("col") + 1) * ring[0].shape[0], axis=0
+    )
     grad_tile = lax.dot_general(
         grads_whole,
         lax.all_gather(activations, "row", axis=0, tiled=True),

time: 1050 us -> 1090 us (1.038)
  local copies, waits for them, and re-layouts: 15 us -> 43.3 us
    ppermute x0 -> x7, waiting for transfers between devices: none -> 176 us  [body(): lax.ppermute(ring[-1], 'col', [(dev, (dev + 1) % 8) for dev in range(8)])]
    all_gather x1 -> x0, waiting for transfers between devices: 127 us -> none  [body(): grads_whole = lax.all_gather(output_grads, 'col', axis=0, tiled=True)]
    all_gather x1, waiting for transfers between devices: 37.3 us -> 0.01 us  [body(): lax.all_gather(activations, 'row', axis=0, tiled=True)]
    unnamed x4 -> x33, local copies, waits for them, and re-layouts: 3.22 us -> 30.6 us
  transfers between devices with their start and end apart: 7 -> 13, of which waited for: 5 -> 10; matrix products, arithmetic and copies ran while one was open for 4% -> 6% of each run, Pallas kernels for 0% -> 0%
where the time goes in v1:
time: 1090 us; the launch traced here: 1080 us
  waiting for transfers between devices  522 us (48%)
  matrix products  323 us (30%)
  other arithmetic  134 us (12%)
  local copies, waits for them, and re-layouts  43.3 us (4%)
  blocking collectives  39.7 us (4%)
  between operations  17.4 us (2%)
    psum x1, waiting for transfers between devices, body(): left_factor = lax.psum(left_partial, 'col')  266 us
    ppermute x7, waiting for transfers between devices, body(): lax.ppermute(ring[-1], 'col', [(dev, (dev + 1) % 8) for dev in range(8)])  176 us
    dot_general x3, matrix products, outer_rows(): lax.dot_general(first, second, (((1,), (1,)), ((), ())), precision=FULL_P...  139 us
    another operation x14, other arithmetic, orthogonalize(): lower_factor = jnp.linalg.cholesky(gram_matrix)  87.5 us
    dot_general x2, matrix products, contract_rows(): lax.dot_general(first, second, (((0,), (0,)), ((), ())), precision=FULL_P...  77.1 us
    dot_general x1, matrix products, body(): jnp.dot(buffer, factor_block, precision=FULL_PRECISION, preferred_element...  65.1 us
    reduce_scatter x1, waiting for transfers between devices, body(): lax.psum_scatter(contract_rows(buffer, ortho_left), 'row', scatter_dimens...  45.2 us
    another operation x3, other arithmetic, orthogonalize(): jax.scipy.linalg.solve_triangular(lower_factor, identity, lower=True)  40.3 us
  transfers between devices with their start and end apart: 13, of which 10 were waited for; matrix products, arithmetic and copies ran while one was open for 6% of the time, Pallas kernels for 0%

profile of v1, /device:TPU:0, one launch (start us, length us, event | category | flops | bytes accessed | tf_op | source)
XLA Modules:
  0.0 1082.5 jit_solution(17393228142728730800)
XLA Ops:
  10.3 26.3 %collective-permute-done = bf16[128,4096]{1,0:T(8,128)(2,1)S(1)} collective-permute-done((bf16[128,4096]{1,0:T(8,128)(2,1)}, bf16[128,4096]{1,0:T(8,128)(2,1)S(1)}, u32[]{:S(2)}, u32[]{:S(2)}) %collective-permute-start) | collective-permute-done | bytes 1048608 | tf_op jit(solution)/shard_map/ppermute | solution.py:45
  36.7 27.0 %collective-permute-done.1 = bf16[128,4096]{1,0:T(8,128)(2,1)S(1)} collective-permute-done((bf16[128,4096]{1,0:T(8,128)(2,1)S(1)}, bf16[128,4096]{1,0:T(8,128)(2,1)S(1)}, u32[]{:S(2)}, u32[]{:S(2)}) %collective-permute-start.1) | collective-permute-done | bytes 1048608 | tf_op jit(solution)/shard_map/ppermute | solution.py:45
  63.7 26.2 %collective-permute-done.2 = bf16[128,4096]{1,0:T(8,128)(2,1)S(1)} collective-permute-done((bf16[128,4096]{1,0:T(8,128)(2,1)S(1)}, bf16[128,4096]{1,0:T(8,128)(2,1)S(1)}, u32[]{:S(2)}, u32[]{:S(2)}) %collective-permute-start.2) | collective-permute-done | bytes 1048608 | tf_op jit(solution)/shard_map/ppermute | solution.py:45
  90.9 25.3 %collective-permute-done.3 = bf16[128,4096]{1,0:T(8,128)(2,1)S(1)} collective-permute-done((bf16[128,4096]{1,0:T(8,128)(2,1)S(1)}, bf16[128,4096]{1,0:T(8,128)(2,1)S(1)}, u32[]{:S(2)}, u32[]{:S(2)}) %collective-permute-start.3) | collective-permute-done | bytes 1048608 | tf_op jit(solution)/shard_map/ppermute | solution.py:45
  117.2 24.4 %collective-permute-done.4 = bf16[128,4096]{1,0:T(8,128)(2,1)S(1)} collective-permute-done((bf16[128,4096]{1,0:T(8,128)(2,1)S(1)}, bf16[128,4096]{1,0:T(8,128)(2,1)S(1)}, u32[]{:S(2)}, u32[]{:S(2)}) %collective-permute-start.4) | collective-permute-done | bytes 1048608 | tf_op jit(solution)/shard_map/ppermute | solution.py:45
  142.6 23.7 %collective-permute-done.5 = bf16[128,4096]{1,0:T(8,128)(2,1)} collective-permute-done((bf16[128,4096]{1,0:T(8,128)(2,1)S(1)}, bf16[128,4096]{1,0:T(8,128)(2,1)}, u32[]{:S(2)}, u32[]{:S(2)}) %collective-permute-start.5) | collective-permute-done | bytes 1048608 | tf_op jit(solution)/shard_map/ppermute | solution.py:45
  166.5 22.9 %collective-permute-done.6 = bf16[128,4096]{1,0:T(8,128)(2,1)} collective-permute-done((bf16[128,4096]{1,0:T(8,128)(2,1)}, bf16[128,4096]{1,0:T(8,128)(2,1)}, u32[]{:S(2)}, u32[]{:S(2)}) %collective-permute-start.6) | collective-permute-done | bytes 1048608 | tf_op jit(solution)/shard_map/ppermute | solution.py:45
  214.8 36.0 %convolution_add_fusion = f32[4096,2048]{1,0:T(8,128)} fusion(f32[4096,2048]{1,0:T(8,128)} %param.6, bf16[1024,2048]{1,0:T(8,128)(2,1)} %all-gather.4.cloned.1.call-done, bf16[2048,4096]{1,0:T(8,128)(2,1)} %constant_dynamic-update-slice_fusion, s32[]{:T(128)S(6)} %select_n.18), kind=kOutput, calls=%fused_computation.4 | convolution fusion | flops 17188257792 | bytes 79691776 | tf_op jit(solution)/shard_map/dot_general | solution.py:49
  250.8 65.1 %fusion.45 = f32[4096,512]{1,0:T(8,128)} fusion(f32[4096,2048]{1,0:T(8,128)} %convolution_add_fusion, f32[2048,512]{1,0:T(8,128)} %all-gather.6.cloned.1.call-done), kind=kOutput, calls=%fused_computation.103 | convolution fusion | flops 51539607552 | bytes 46137344 | tf_op jit(solution)/shard_map/dot_general | solution.py:57
  316.2 266.1 %all-reduce.4.cloned.1.call-done = f32[4096,512]{1,0:T(8,128)} async-done(((f32[4096,512]{1,0:T(8,128)}), f32[4096,512]{1,0:T(8,128)}) %all-reduce.4.cloned.1.call-update) | async-done | bytes 8388624 | tf_op jit(solution)/shard_map/psum | solution.py:60
  582.3 18.3 %fusion.46 = f32[512,512]{0,1:T(8,128)} fusion(f32[4096,512]{1,0:T(8,128)} %all-reduce.4.cloned.1.call-done), kind=kOutput, calls=%fused_computation.104 | convolution fusion | flops 12884901888 | bytes 9437184 | tf_op jit(solution)/shard_map/dot_general | solution.py:16
  601.6 34.6 %all-reduce.6.cloned.1.call-done = f32[512,512]{0,1:T(8,128)} async-done(((f32[512,512]{0,1:T(8,128)}), f32[512,512]{0,1:T(8,128)}) %all-reduce.6.cloned.1.call-update) | async-done | bytes 1048592 | tf_op jit(solution)/shard_map/psum | solution.py:61
  639.2 11.7 %cholesky.104 = f32[128,128]{1,0:T(8,128)S(1)} custom-call(f32[128,128]{1,0:T(8,128)S(1)} %cholesky.266), custom_call_target="Cholesky" | custom-call | tf_op jit(solution)/shard_map/jit(cholesky)/cholesky | solution.py:36
  661.6 11.7 %cholesky.217 = f32[128,128]{1,0:T(8,128)S(1)} custom-call(f32[128,128]{1,0:T(8,128)S(1)} %cholesky.270), custom_call_target="Cholesky" | custom-call | tf_op jit(solution)/shard_map/jit(cholesky)/cholesky | solution.py:36
  673.3 18.5 %custom-call.32 = f32[1,128,128]{1,2,0:T(8,128)S(1)} custom-call(f32[1,128,128]{2,1,0:T(8,128)S(1)} %get-tuple-element.27), custom_call_target="InvertDiagBlocksLowerTriangular" | custom-call | tf_op jit(solution)/shard_map/jit(cholesky)/cholesky | solution.py:36
  692.5 11.7 %cholesky.238 = f32[128,128]{1,0:T(8,128)S(1)} custom-call(f32[128,128]{1,0:T(8,128)S(1)} %cholesky.275), custom_call_target="Cholesky" | custom-call | tf_op jit(solution)/shard_map/jit(cholesky)/cholesky | solution.py:36
  715.3 11.7 %cholesky.255 = f32[128,128]{1,0:T(8,128)S(1)} custom-call(f32[128,128]{1,0:T(8,128)S(1)} %convolution_subtract_fusion.5), custom_call_target="Cholesky" | custom-call | tf_op jit(solution)/shard_map/jit(cholesky)/cholesky | solution.py:36
  741.5 40.1 %custom-call.34 = f32[4,128,128]{1,2,0:T(8,128)S(1)} custom-call(f32[4,128,128]{2,1,0:T(8,128)} %get-tuple-element.10), custom_call_target="InvertDiagBlocksLowerTriangular" | custom-call | tf_op jit(solution)/shard_map/jit(_solve_triangular)/triangular_solve | solution.py:38
  785.4 17.1 %fusion.3 = f32[4096,512]{1,0:T(8,128)S(1)} fusion(f32[4096,512]{1,0:T(8,128)} %all-reduce.4.cloned.1.call-done, f32[128,512]{1,0:T(8,128)S(1)} %fusion.31, f32[128,512]{1,0:T(8,128)S(1)} %fusion.32, f32[128,512]{1,0:T(8,128)S(1)} %fusion.34, f32[128,512]{1,0:T(8,128)S(1)} %fusion.22), kind=kOutput, calls=%fused_computation.17 | convolution fusion | flops 12885688320 | bytes 17825792 | tf_op jit(solution)/shard_map/dot_general | solution.py:26
  805.8 58.7 %fusion.47 = f32[2048,512]{1,0:T(8,128)} fusion(f32[4096,2048]{1,0:T(8,128)} %convolution_add_fusion, f32[4096,512]{1,0:T(8,128)S(1)} %fusion.3), kind=kOutput, calls=%fused_computation.105 | convolution fusion | flops 51539607552 | bytes 46137344 | tf_op jit(solution)/shard_map/dot_general | solution.py:16
  864.6 45.2 %reduce-scatter.2.cloned.1.call-done = f32[512,512]{1,0:T(8,128)} async-done(((f32[2048,512]{1,0:T(8,128)}), f32[512,512]{1,0:T(8,128)}) %reduce-scatter.2.cloned.1.call-update) | async-done | bytes 1048592 | tf_op jit(solution)/shard_map/reduce_scatter | solution.py:63
  911.1 39.7 %psum.23 = f32[512]{0:T(512)S(1)} all-reduce(f32[512]{0:T(512)S(1)} %multiply_reduce_fusion), channel_id=1, replica_groups=mesh['row'=4,'col'=8] {'row','col'}, use_global_device_ids=true, to_apply=%region_12.13 | all-reduce | flops 512 | bytes 4096 | tf_op jit(solution)/shard_map/psum | solution.py:66
  953.1 62.5 %multiply_subtract_fusion = f32[4096,2048]{1,0:T(8,128)} fusion(f32[4096,2048]{1,0:T(8,128)} %convolution_add_fusion, f32[4096,512]{1,0:T(8,128)} %copy-done, f32[2048,512]{1,0:T(8,128)} %all-gather.8.cloned.1.call-done), kind=kOutput, calls=%fused_computation.2 | convolution fusion | flops 51556384768 | bytes 79691776 | tf_op jit(solution)/shard_map/dot_general | solution.py:26
  1015.6 59.6 %subtract_convert_fusion = bf16[4096,2048]{1,0:T(8,128)(2,1)} fusion(bf16[4096,2048]{1,0:T(8,128)(2,1)} %param.5, f32[4096,512]{1,0:T(8,128)} %copy-done, f32[2048,512]{1,0:T(8,128)S(1)} %copy-done.1, f32[512]{0:T(512)S(1)} %add_sqrt_fusion), kind=kOutput, calls=%fused_computation.3 | convolution fusion | flops 51574210560 | bytes 46139392 | tf_op jit(solution)/shard_map/dot_general | solution.py:26
  (106 shorter events, 91.0 us)
Async XLA Ops:
  7.2 195.8 %copy-start.2 = (bf16[128,4096]{1,0:T(8,128)(2,1)S(1)}, bf16[128,4096]{1,0:T(8,128)(2,1)}, u32[]{:S(2)}) copy-start(bf16[128,4096]{1,0:T(8,128)(2,1)} %param.8) | copy-start | bytes 3145732
  7.2 207.6 %all-gather.4.cloned.1.call-start = ((), (), s32[]{:S(2)}) async-start(), calls=%async_computation.1 | async-start | bytes 5242880 | tf_op jit(solution)/shard_map/all_gather | solution.py:51
  7.2 29.5 %collective-permute-start = (bf16[128,4096]{1,0:T(8,128)(2,1)}, bf16[128,4096]{1,0:T(8,128)(2,1)S(1)}, u32[]{:S(2)}, u32[]{:S(2)}) collective-permute-start(bf16[128,4096]{1,0:T(8,128)(2,1)} %param.8), channel_id=1, source_target_pairs={{0,1},{1,2},{2,3},{3,4},{4,5},{5,6},{6,7},{7,0},{8,9},{9,10},{10,1... | collective-permute-start | bytes 3145736 | tf_op jit(solution)/shard_map/ppermute | solution.py:45
  10.3 240.5 %all-gather.6.cloned.1.call-start = ((), (), s32[]{:S(2)}) async-start(), calls=%async_computation.2 | async-start | bytes 5242880 | tf_op jit(solution)/shard_map/all_gather | solution.py:56
  36.7 27.0 %collective-permute-start.1 = (bf16[128,4096]{1,0:T(8,128)(2,1)S(1)}, bf16[128,4096]{1,0:T(8,128)(2,1)S(1)}, u32[]{:S(2)}, u32[]{:S(2)}) collective-permute-start(bf16[128,4096]{1,0:T(8,128)(2,1)S(1)} %collective-permute-done), channel_id=1, source_target_pairs={{0,1},{1,2},{2,3},{3,4},{4,5},{5,6},{6,7},{7,0},{8,9},{9,10},{10,1... | collective-permute-start | bytes 3145736 | tf_op jit(solution)/shard_map/ppermute | solution.py:45
  63.7 26.2 %collective-permute-start.2 = (bf16[128,4096]{1,0:T(8,128)(2,1)S(1)}, bf16[128,4096]{1,0:T(8,128)(2,1)S(1)}, u32[]{:S(2)}, u32[]{:S(2)}) collective-permute-start(bf16[128,4096]{1,0:T(8,128)(2,1)S(1)} %collective-permute-done.1), channel_id=1, source_target_pairs={{0,1},{1,2},{2,3},{3,4},{4,5},{5,6},{6,7},{7,0},{8,9},{9,10},{10,1... | collective-permute-start | bytes 3145736 | tf_op jit(solution)/shard_map/ppermute | solution.py:45
  89.9 1.1 copy-start.3
  90.9 25.3 %collective-permute-start.3 = (bf16[128,4096]{1,0:T(8,128)(2,1)S(1)}, bf16[128,4096]{1,0:T(8,128)(2,1)S(1)}, u32[]{:S(2)}, u32[]{:S(2)}) collective-permute-start(bf16[128,4096]{1,0:T(8,128)(2,1)S(1)} %collective-permute-done.2), channel_id=1, source_target_pairs={{0,1},{1,2},{2,3},{3,4},{4,5},{5,6},{6,7},{7,0},{8,9},{9,10},{10,1... | collective-permute-start | bytes 3145736 | tf_op jit(solution)/shard_map/ppermute | solution.py:45
  116.2 1.0 copy-start.5
  117.2 24.5 %collective-permute-start.4 = (bf16[128,4096]{1,0:T(8,128)(2,1)S(1)}, bf16[128,4096]{1,0:T(8,128)(2,1)S(1)}, u32[]{:S(2)}, u32[]{:S(2)}) collective-permute-start(bf16[128,4096]{1,0:T(8,128)(2,1)S(1)} %collective-permute-done.3), channel_id=1, source_target_pairs={{0,1},{1,2},{2,3},{3,4},{4,5},{5,6},{6,7},{7,0},{8,9},{9,10},{10,1... | collective-permute-start | bytes 3145736 | tf_op jit(solution)/shard_map/ppermute | solution.py:45
  141.6 1.0 copy-start.7
  142.6 23.7 %collective-permute-start.5 = (bf16[128,4096]{1,0:T(8,128)(2,1)S(1)}, bf16[128,4096]{1,0:T(8,128)(2,1)}, u32[]{:S(2)}, u32[]{:S(2)}) collective-permute-start(bf16[128,4096]{1,0:T(8,128)(2,1)S(1)} %collective-permute-done.4), channel_id=1, source_target_pairs={{0,1},{1,2},{2,3},{3,4},{4,5},{5,6},{6,7},{7,0},{8,9},{9,10},{10,1... | collective-permute-start | bytes 3145736 | tf_op jit(solution)/shard_map/ppermute | solution.py:45
  166.3 23.1 %collective-permute-start.6 = (bf16[128,4096]{1,0:T(8,128)(2,1)}, bf16[128,4096]{1,0:T(8,128)(2,1)}, u32[]{:S(2)}, u32[]{:S(2)}) collective-permute-start(bf16[128,4096]{1,0:T(8,128)(2,1)} %collective-permute-done.5), channel_id=1, source_target_pairs={{0,1},{1,2},{2,3},{3,4},{4,5},{5,6},{6,7},{7,0},{8,9},{9,10},{10,1... | collective-permute-start | bytes 3145736 | tf_op jit(solution)/shard_map/ppermute | solution.py:45
  166.3 415.9 %all-reduce.4.cloned.1.call-start = ((), (), s32[]{:S(2)}) async-start(), calls=%async_computation.3 | async-start | bytes 16777216 | tf_op jit(solution)/shard_map/psum | solution.py:60
  166.4 42.1 %copy-start.8 = (bf16[128,4096]{1,0:T(8,128)(2,1)S(1)}, bf16[128,4096]{1,0:T(8,128)(2,1)}, u32[]{:S(2)}) copy-start(bf16[128,4096]{1,0:T(8,128)(2,1)} %copy-done.7) | copy-start | bytes 3145732
  166.4 43.2 %copy-start.6 = (bf16[128,4096]{1,0:T(8,128)(2,1)S(1)}, bf16[128,4096]{1,0:T(8,128)(2,1)}, u32[]{:S(2)}) copy-start(bf16[128,4096]{1,0:T(8,128)(2,1)} %copy-done.5) | copy-start | bytes 3145732
  166.4 44.2 %copy-start.4 = (bf16[128,4096]{1,0:T(8,128)(2,1)S(1)}, bf16[128,4096]{1,0:T(8,128)(2,1)}, u32[]{:S(2)}) copy-start(bf16[128,4096]{1,0:T(8,128)(2,1)} %copy-done.3) | copy-start | bytes 3145732
  315.9 320.3 %all-reduce.6.cloned.1.call-start = ((), (), s32[]{:S(2)}) async-start(), calls=%async_computation.4 | async-start | bytes 2097152 | tf_op jit(solution)/shard_map/psum | solution.py:61
  600.6 309.1 %reduce-scatter.2.cloned.1.call-start = ((), (), s32[]{:S(2)}) async-start(), calls=%async_computation.5 | async-start | bytes 5242880 | tf_op jit(solution)/shard_map/reduce_scatter | solution.py:63
  802.5 3.2 copy-start
  864.5 88.6 %all-gather.8.cloned.1.call-start = ((), (), s32[]{:S(2)}) async-start(), calls=%async_computation.6 | async-start | bytes 5242880 | tf_op jit(solution)/shard_map/all_gather | solution.py:69
  953.1 62.5 %copy-start.1 = (f32[2048,512]{1,0:T(8,128)S(1)}, f32[2048,512]{1,0:T(8,128)}, u32[]{:S(2)}) copy-start(f32[2048,512]{1,0:T(8,128)} %all-gather.8.cloned.1.call-done) | copy-start | bytes 12582916
Sparse Core Ops, SparseCore 0:
  10.4 36.2 all-gather.3
  166.5 35.0 all-gather.5
  316.0 266.2 all-reduce.3
  600.8 35.3 all-reduce.5
  864.7 45.0 reduce-scatter.1
  911.2 34.7 all-gather.7
